TPU v7x, 256 devices: a whole 4x4x8 slice. The times are simulated.
256 devices in a mesh: agents: 64 (over z, x, core), group: 4 (over y).
Axes of the slice: x: 4, y: 4, z: 8, core: 2. Of those that a mesh axis runs over, the one named last changes fastest.
Arguments:
- q_lin: float32 [4, 40, 16384], P('group', None, 'agents'), may hold values from -6 to 6
- inverse: bfloat16 [4, 40, 40, 16384], P('group', None, None, 'agents'), may hold values from -0.5 to 1, as said below
- predict: bfloat16 [4, 40, 40, 16384], P('group', None, None, 'agents'), may hold values from -1 to 1
- free_traj: float32 [4, 40, 16384], P('group', None, 'agents'), may hold values from -6 to 6
- offsets: float32 [4, 8, 40, 16384], P('group', None, None, 'agents'), may hold values from -4 to 4
- multipliers: float32 [4, 8, 40, 16384], P('group', None, None, 'agents'), may hold values from -4 to 4
- nbr_owner: int32 [4, 8, 16384], P('group', None, 'agents'), may hold values from 0 to 63, as said below
- nbr_slot: int32 [4, 8, 16384], P('group', None, 'agents'), may hold values from -1 to 255
- platoon: int32 [4, 16384], P('group', 'agents'), may hold values from 0 to 127, as said below
Outputs:
- inputs_plan: float32 [4, 40, 16384], P('group', None, 'agents')
- multipliers_out: float32 [4, 8, 40, 16384], P('group', None, None, 'agents')
Inputs may be any that keep to these rules, and one draw needn't show every extreme that they name: `nbr_owner`: an agent's own block index is its row in the region // 256; each neighbour's owner lies within 2 blocks of it, slot 0 is never padded. `inverse`: symmetric for every agent. `platoon`: 32 or more platoons hold no agent of any region.
All inputs are finite; a program needn't handle non-finite values. Where the computation divides by a largest or mean magnitude, that divisor is 1e-20 or more.
Results may differ from a plain program's by a relative error of at most 0.0003.
Values sent between devices are 32-bit elements; how exact they have to be, the bound alone decides.
A program may use at most 64 MiB of HBM per device.

v0:
```python
import functools

import jax
import jax.numpy as jnp
from jax import lax
from jax.sharding import Mesh
from jax.sharding import PartitionSpec as P

SPAN = 2
NPLAT = 128
ITERS = 3
AGENTS = ("agents_0", "agents_1", "agents_2")
AGENTS_GROUP = ("agents_0", "agents_1", "agents_2", "group")


RHO = 0.5
KAPPA = 0.5


def shifted(value, axis, steps):
    count = lax.axis_size(axis)
    first, last = (max(0, -steps), min(count, count - steps))
    return lax.ppermute(value, axis, [(source, source + steps) for source in range(first, last)])


def over_axes(x, axes):
    return functools.reduce(lax.psum, axes, x)


def all_in_one(x, axis):
    leaves = jax.tree.leaves(x)
    sequence = sorted(range(len(leaves)), key=lambda k: -leaves[k].size)
    width = (1, *leaves[sequence[0]].shape)[-1]
    lines = [
        jnp.pad(leaves[k].reshape(-1), (0, -leaves[k].size % width)).reshape(-1, width)
        for k in sequence
    ]
    both, at, found = (lax.all_gather(jnp.concatenate(lines), axis), 0, {})
    for k, line in zip(sequence, lines):
        section = both[:, at : at + len(line)].reshape(len(both), -1)
        found[k] = section[:, : leaves[k].size].reshape(-1, *leaves[k].shape)
        at += len(line)
    numbers = iter(range(len(leaves)))
    return jax.tree.map(lambda _: found[next(numbers)], x)


def once_a_type(x, axis):
    leaves, found = (jax.tree.leaves(x), {})
    for first, a in enumerate(leaves):
        if first not in found:
            alike = [k for k, b in enumerate(leaves) if b.dtype == a.dtype]
            got = (
                all_in_one([leaves[k] for k in alike], axis)
                if len(alike) > 1
                else [lax.all_gather(a, axis)]
            )
            for k, b in zip(alike, got):
                found[k] = b
    numbers = iter(range(len(leaves)))
    return jax.tree.map(lambda _: found[next(numbers)], x)


def joined_all(x, axes, combine):
    for axis in axes:
        pieces = once_a_type(x, axis)
        x = jax.tree.map(lambda part: part[0], pieces)
        for k in range(1, lax.axis_size(axis)):
            x = combine(x, jax.tree.map(lambda part: part[k], pieces))
    return x


def by_axis(x, axes):
    return functools.reduce(lax.pmax, axes, x)


def combine_stats(first, second):
    return (first[0] + second[0], jnp.maximum(first[1], second[1]))


def local(q_lin, inverse, predict, free_traj, offsets, multipliers, nbr_owner, nbr_slot, platoon):
    block = q_lin.shape[2]
    traj_len = free_traj.shape[1]
    alive = nbr_slot >= 0
    live = alive.astype(jnp.float32)[:, :, None, :]
    onehot = (platoon[:, None, :] == jnp.arange(NPLAT, dtype=jnp.int32)[None, :, None]).astype(
        jnp.float32
    )
    counts_local = jnp.sum(onehot, axis=(0, 2))
    mine = lax.axis_index(AGENTS)
    column = (nbr_owner - mine + SPAN) * block + nbr_slot
    column = jnp.where(alive, column, 0)[0].reshape(-1)

    def lookup(field):
        pieces = []
        for distance in range(-SPAN, SPAN + 1):
            if distance == 0:
                pieces.append(field)
            else:
                pieces.append(shifted(field, AGENTS, -distance))
        joined = jnp.concatenate(pieces, axis=2)
        taken = jnp.take(joined[0], column, axis=1).reshape(traj_len, nbr_slot.shape[1], block)
        return jnp.transpose(taken, (1, 0, 2))[None] * live

    def platoon_local(field):
        return jnp.einsum("rta,rpa->tp", field, onehot, precision=lax.Precision.HIGHEST)

    traj = free_traj
    lam = multipliers
    near = lookup(traj)
    sums, counts = (
        over_axes(platoon_local(traj), AGENTS_GROUP),
        over_axes(counts_local, AGENTS_GROUP),
    )
    divisor = jnp.maximum(counts, 1.0)[None, :]

    def spread(totals):
        means = totals / divisor
        return jnp.einsum("tp,rpa->rta", means, onehot, precision=lax.Precision.HIGHEST)

    attract = spread(sums)
    plan = jnp.zeros_like(q_lin)
    for step in range(ITERS):
        coupling = jnp.sum(live * (lam - RHO * (near + offsets)), axis=1) - KAPPA * attract
        rhs = q_lin + jnp.einsum(
            "rtja,rta->rja", predict.astype(jnp.float32), coupling, precision=lax.Precision.HIGHEST
        )
        plan = -jnp.einsum(
            "rija,rja->ria", inverse.astype(jnp.float32), rhs, precision=lax.Precision.HIGHEST
        )
        traj = (
            jnp.einsum(
                "rtja,rja->rta", predict.astype(jnp.float32), plan, precision=lax.Precision.HIGHEST
            )
            + free_traj
        )
        near = lookup(traj)
        gap = live * (traj[:, None] - near - offsets)
        local_peak = jnp.max(jnp.abs(gap))
        more = step + 1 < ITERS
        if more:
            sums, peak = joined_all((platoon_local(traj), local_peak), AGENTS_GROUP, combine_stats)
        else:
            peak = by_axis(local_peak, AGENTS_GROUP)
        lam = lam + gap / (1.0 + peak)
        if more:
            attract = spread(sums)
    return (plan, lam)


def solution(mesh):
    finer = Mesh(
        mesh.devices.reshape(8, 4, 2, mesh.shape["group"]),
        ("agents_0", "agents_1", "agents_2", "group"),
    )
    placed = (
        P("group", None, AGENTS),
        P("group", None, None, AGENTS),
        P("group", None, None, AGENTS),
        P("group", None, AGENTS),
        P("group", None, None, AGENTS),
        P("group", None, None, AGENTS),
        P("group", None, AGENTS),
        P("group", None, AGENTS),
        P("group", AGENTS),
    )
    return jax.shard_map(
        local,
        mesh=finer,
        in_specs=placed,
        out_specs=(P("group", None, AGENTS), P("group", None, None, AGENTS)),
        check_vma=False,
    )
```

profile of v0, /device:TPU:1, one launch (start us, length us, event | category | flops | bytes accessed | tf_op | source)
XLA Modules:
  0.0 351.5 jit_solution(14953525643626272424)
XLA Ops:
  0.6 3.9 %collective-permute-start = (f32[1,40,256]{2,1,0:T(8,128)}, f32[1,40,256]{2,1,0:T(8,128)S(1)}, u32[]{:S(2)}, u32[]{:S(2)}) collective-permute-start(f32[1,40,256]{2,1,0:T(8,128)} %param.14), channel_id=1, source_target_pairs={{0,8},{4,12},{8,16},{12,20},{16,24},{20,28},{24,32},{28,36},{32,40... | collective-permute-start | bytes 122888 | tf_op jit(solution)/shard_map/ppermute | solution.py:23
  4.6 4.0 %collective-permute-start.1 = (f32[1,40,256]{2,1,0:T(8,128)}, f32[1,40,256]{2,1,0:T(8,128)S(1)}, u32[]{:S(2)}, u32[]{:S(2)}) collective-permute-start(f32[1,40,256]{2,1,0:T(8,128)} %param.14), channel_id=1, source_target_pairs={{0,4},{4,8},{8,12},{12,16},{16,20},{20,24},{24,28},{28,32},{32,36}... | collective-permute-start | bytes 122888 | tf_op jit(solution)/shard_map/ppermute | solution.py:23
  8.5 1.9 collective-permute-start.2
  10.5 1.3 collective-permute-start.3
  11.8 1.0 convolution_bitcast_fusion
  15.0 28.5 %all-reduce.8 = (f32[40,128]{1,0:T(8,128)S(1)}, f32[128]{0:T(128)S(1)}) all-reduce(f32[40,128]{1,0:T(8,128)S(1)} %convolution_bitcast_fusion, f32[128]{0:T(128)S(1)} %convert_reduce_fusion), channel_id=1, replica_groups=mesh['agents_0'=8,'agents_1'=4,'agents_2'=2,'group'=4] {'agents_0'}, use_global_device_ids=true, to_apply=%region_1.3 | all-reduce | flops 5248 | bytes 41984 | tf_op jit(solution)/shard_map/psum | solution.py:27
  43.6 10.9 %all-reduce.10 = (f32[40,128]{1,0:T(8,128)S(1)}, f32[128]{0:T(128)S(1)}) all-reduce(f32[40,128]{1,0:T(8,128)S(1)} %get-tuple-element.3, f32[128]{0:T(128)S(1)} %get-tuple-element.4), channel_id=1, replica_groups=mesh['agents_0'=8,'agents_1'=4,'agents_2'=2,'group'=4] {'agents_1'}, use_global_device_ids=true, to_apply=%region_2.4 | all-reduce | flops 5248 | bytes 41984 | tf_op jit(solution)/shard_map/psum | solution.py:27
  54.5 16.2 %all-reduce.11 = (f32[40,128]{1,0:T(8,128)S(1)}, f32[128]{0:T(128)S(1)}) all-reduce(f32[40,128]{1,0:T(8,128)S(1)} %get-tuple-element.7, f32[128]{0:T(128)S(1)} %get-tuple-element.8), channel_id=1, replica_groups=mesh['agents_0'=8,'agents_1'=4,'agents_2'=2,'group'=4] {'agents_2'}, use_global_device_ids=true, to_apply=%region_3.5 | all-reduce | flops 5248 | bytes 41984 | tf_op jit(solution)/shard_map/psum | solution.py:27
  70.7 13.5 %all-reduce.9 = (f32[40,128]{1,0:T(8,128)S(1)}, f32[128]{0:T(128)S(1)}) all-reduce(f32[40,128]{1,0:T(8,128)S(1)} %get-tuple-element.9, f32[128]{0:T(128)S(1)} %get-tuple-element.10), channel_id=1, replica_groups=mesh['agents_0'=8,'agents_1'=4,'agents_2'=2,'group'=4] {'group'}, use_global_device_ids=true, to_apply=%region_4.6 | all-reduce | flops 5248 | bytes 41984 | tf_op jit(solution)/shard_map/psum | solution.py:27
  85.4 5.5 %gather_fusion = f32[2048,40]{1,0:T(8,128)S(1)} fusion(f32[40,1280]{0,1:T(8,128)S(1)} %bitcast.324, s32[2048]{0:T(1024)S(1)} %fusion.63), kind=kCustom, calls=%fused_computation.clone | custom fusion | bytes 663552 | tf_op jit(solution)/shard_map/jit(_take)/gather | solution.py:101
  94.3 1.3 collective-permute-start.4
  95.6 7.5 %collective-permute-start.5 = (f32[1,40,256]{2,1,0:T(8,128)S(1)}, f32[1,40,256]{2,1,0:T(8,128)S(1)}, u32[]{:S(2)}, u32[]{:S(2)}) collective-permute-start(f32[1,40,256]{2,1,0:T(8,128)S(1)} %bitcast_add_fusion.7), channel_id=1, source_target_pairs={{0,4},{4,8},{8,12},{12,16},{16,20},{20,24},{24,28},{28,32},{32,36}... | collective-permute-start | bytes 122888 | tf_op jit(solution)/shard_map/ppermute | solution.py:23
  103.0 1.9 collective-permute-start.6
  105.0 1.3 collective-permute-start.7
  106.5 1.8 collective-permute-done.6
  108.4 1.3 collective-permute-done.7
  110.0 7.6 %gather_fusion.1 = f32[2048,40]{1,0:T(8,128)} fusion(f32[40,1280]{0,1:T(8,128)S(1)} %bitcast.325, s32[2048]{0:T(1024)S(1)} %fusion.63), kind=kCustom, calls=%fused_computation.1.clone | custom fusion | bytes 663552 | tf_op jit(solution)/shard_map/jit(_take)/gather | solution.py:101
  117.5 1.6 broadcast_select_fusion.2
  120.8 19.2 %all-gather.8 = f32[8,41,128]{2,1,0:T(8,128)S(1)} all-gather(f32[1,41,128]{2,1,0:T(8,128)S(1)} %maximum_bitcast_fusion), channel_id=2, replica_groups=mesh['agents_0'=8,'agents_1'=4,'agents_2'=2,'group'=4] {'agents_0'}, dimensions={0}, use_global_device_ids=true | all-gather | bytes 188928 | tf_op jit(solution)/shard_map/all_gather | solution.py:38
  145.7 9.1 %all-gather.9 = f32[4,41,128]{2,1,0:T(8,128)S(1)} all-gather(f32[1,41,128]{2,1,0:T(8,128)S(1)} %maximum_bitcast_fusion.1), channel_id=3, replica_groups=mesh['agents_0'=8,'agents_1'=4,'agents_2'=2,'group'=4] {'agents_1'}, dimensions={0}, use_global_device_ids=true | all-gather | bytes 104960 | tf_op jit(solution)/shard_map/all_gather | solution.py:38
  158.0 13.0 %all-gather.10 = f32[2,41,128]{2,1,0:T(8,128)S(1)} all-gather(f32[1,41,128]{2,1,0:T(8,128)S(1)} %maximum_bitcast_fusion.2), channel_id=4, replica_groups=mesh['agents_0'=8,'agents_1'=4,'agents_2'=2,'group'=4] {'agents_2'}, dimensions={0}, use_global_device_ids=true | all-gather | bytes 62976 | tf_op jit(solution)/shard_map/all_gather | solution.py:38
  172.9 9.0 %all-gather.11 = f32[4,41,128]{2,1,0:T(8,128)S(1)} all-gather(f32[1,41,128]{2,1,0:T(8,128)S(1)} %maximum_bitcast_fusion.3), channel_id=5, replica_groups=mesh['agents_0'=8,'agents_1'=4,'agents_2'=2,'group'=4] {'group'}, dimensions={0}, use_global_device_ids=true | all-gather | bytes 104960 | tf_op jit(solution)/shard_map/all_gather | solution.py:38
  186.3 3.6 %collective-permute-start.8 = (f32[1,40,256]{2,1,0:T(8,128)S(1)}, f32[1,40,256]{2,1,0:T(8,128)S(1)}, u32[]{:S(2)}, u32[]{:S(2)}) collective-permute-start(f32[1,40,256]{2,1,0:T(8,128)S(1)} %bitcast_add_fusion.5), channel_id=1, source_target_pairs={{0,8},{4,12},{8,16},{12,20},{16,24},{20,28},{24,32},{28,36},{32,40... | collective-permute-start | bytes 122888 | tf_op jit(solution)/shard_map/ppermute | solution.py:23
  189.9 5.0 %collective-permute-start.9 = (f32[1,40,256]{2,1,0:T(8,128)S(1)}, f32[1,40,256]{2,1,0:T(8,128)S(1)}, u32[]{:S(2)}, u32[]{:S(2)}) collective-permute-start(f32[1,40,256]{2,1,0:T(8,128)S(1)} %bitcast_add_fusion.5), channel_id=1, source_target_pairs={{0,4},{4,8},{8,12},{12,16},{16,20},{20,24},{24,28},{28,32},{32,36}... | collective-permute-start | bytes 122888 | tf_op jit(solution)/shard_map/ppermute | solution.py:23
  195.0 1.9 collective-permute-start.10
  196.9 1.3 collective-permute-start.11
  198.5 1.8 collective-permute-done.10
  200.3 2.4 collective-permute-done.11
  202.9 7.6 %gather_fusion.2 = f32[2048,40]{1,0:T(8,128)} fusion(f32[40,1280]{0,1:T(8,128)S(1)} %bitcast.326, s32[2048]{0:T(1024)S(1)} %fusion.63), kind=kCustom, calls=%fused_computation.2.clone | custom fusion | bytes 663552 | tf_op jit(solution)/shard_map/jit(_take)/gather | solution.py:101
  210.5 1.6 broadcast_select_fusion.1
  212.1 1.0 copy.41
  213.1 1.8 abs_reduce_fusion.1
  215.6 20.7 %all-gather.12 = f32[8,41,128]{2,1,0:T(8,128)S(1)} all-gather(f32[1,41,128]{2,1,0:T(8,128)S(1)} %maximum_bitcast_fusion.4), channel_id=6, replica_groups=mesh['agents_0'=8,'agents_1'=4,'agents_2'=2,'group'=4] {'agents_0'}, dimensions={0}, use_global_device_ids=true | all-gather | bytes 188928 | tf_op jit(solution)/shard_map/all_gather | solution.py:38
  241.9 10.2 %all-gather.13 = f32[4,41,128]{2,1,0:T(8,128)S(1)} all-gather(f32[1,41,128]{2,1,0:T(8,128)S(1)} %maximum_bitcast_fusion.5), channel_id=7, replica_groups=mesh['agents_0'=8,'agents_1'=4,'agents_2'=2,'group'=4] {'agents_1'}, dimensions={0}, use_global_device_ids=true | all-gather | bytes 104960 | tf_op jit(solution)/shard_map/all_gather | solution.py:38
  255.3 12.3 %all-gather.14 = f32[2,41,128]{2,1,0:T(8,128)S(1)} all-gather(f32[1,41,128]{2,1,0:T(8,128)S(1)} %maximum_bitcast_fusion.6), channel_id=8, replica_groups=mesh['agents_0'=8,'agents_1'=4,'agents_2'=2,'group'=4] {'agents_2'}, dimensions={0}, use_global_device_ids=true | all-gather | bytes 62976 | tf_op jit(solution)/shard_map/all_gather | solution.py:38
  269.5 9.0 %all-gather.15 = f32[4,41,128]{2,1,0:T(8,128)S(1)} all-gather(f32[1,41,128]{2,1,0:T(8,128)S(1)} %maximum_bitcast_fusion.7), channel_id=9, replica_groups=mesh['agents_0'=8,'agents_1'=4,'agents_2'=2,'group'=4] {'group'}, dimensions={0}, use_global_device_ids=true | all-gather | bytes 104960 | tf_op jit(solution)/shard_map/all_gather | solution.py:38
  281.7 0.9 fusion.22
  284.1 3.0 collective-permute-start.12
  287.1 5.1 %collective-permute-start.13 = (f32[1,40,256]{2,1,0:T(8,128)S(1)}, f32[1,40,256]{2,1,0:T(8,128)S(1)}, u32[]{:S(2)}, u32[]{:S(2)}) collective-permute-start(f32[1,40,256]{2,1,0:T(8,128)S(1)} %bitcast_add_fusion.3), channel_id=1, source_target_pairs={{0,4},{4,8},{8,12},{12,16},{16,20},{20,24},{24,28},{28,32},{32,36}... | collective-permute-start | bytes 122888 | tf_op jit(solution)/shard_map/ppermute | solution.py:23
  292.2 1.9 collective-permute-start.14
  294.2 1.3 collective-permute-start.15
  295.5 2.0 collective-permute-done.14
  297.6 2.4 collective-permute-done.15
  300.2 5.5 %gather_fusion.3 = f32[2048,40]{1,0:T(8,128)S(1)} fusion(f32[40,1280]{0,1:T(8,128)S(1)} %bitcast.323, s32[2048]{0:T(1024)S(1)} %fusion.63), kind=kCustom, calls=%fused_computation.3.clone | custom fusion | bytes 663552 | tf_op jit(solution)/shard_map/jit(_take)/gather | solution.py:101
  307.1 14.2 %pmax.28 = f32[]{:T(128)} all-reduce(f32[]{:T(128)} %abs_reduce_fusion), channel_id=1, replica_groups=mesh['agents_0'=8,'agents_1'=4,'agents_2'=2,'group'=4] {'agents_0'}, use_global_device_ids=true, to_apply=%region_15.17 | all-reduce | flops 1 | bytes 8 | tf_op jit(solution)/shard_map/pmax | solution.py:73
  321.3 11.0 %pmax.29 = f32[]{:T(128)} all-reduce(f32[]{:T(128)} %pmax.28), channel_id=1, replica_groups=mesh['agents_0'=8,'agents_1'=4,'agents_2'=2,'group'=4] {'agents_1'}, use_global_device_ids=true, to_apply=%region_16.18 | all-reduce | flops 1 | bytes 8 | tf_op jit(solution)/shard_map/pmax | solution.py:73
  332.2 10.9 %pmax.30 = f32[]{:T(128)} all-reduce(f32[]{:T(128)} %pmax.29), channel_id=1, replica_groups=mesh['agents_0'=8,'agents_1'=4,'agents_2'=2,'group'=4] {'agents_2'}, use_global_device_ids=true, to_apply=%region_17.19 | all-reduce | flops 1 | bytes 8 | tf_op jit(solution)/shard_map/pmax | solution.py:73
  343.2 6.8 %pmax.31 = f32[]{:T(128)} all-reduce(f32[]{:T(128)} %pmax.30), channel_id=1, replica_groups=mesh['agents_0'=8,'agents_1'=4,'agents_2'=2,'group'=4] {'group'}, use_global_device_ids=true, to_apply=%region_18.20 | all-reduce | flops 1 | bytes 8 | tf_op jit(solution)/shard_map/pmax | solution.py:73
  (138 shorter events, 19.9 us)
Async XLA Ops:
  0.6 83.6 %collective-permute-start = (f32[1,40,256]{2,1,0:T(8,128)}, f32[1,40,256]{2,1,0:T(8,128)S(1)}, u32[]{:S(2)}, u32[]{:S(2)}) collective-permute-start(f32[1,40,256]{2,1,0:T(8,128)} %param.14), channel_id=1, source_target_pairs={{0,8},{4,12},{8,16},{12,20},{16,24},{20,28},{24,32},{28,36},{32,40... | collective-permute-start | bytes 122888 | tf_op jit(solution)/shard_map/ppermute | solution.py:23
  4.6 79.7 %collective-permute-start.1 = (f32[1,40,256]{2,1,0:T(8,128)}, f32[1,40,256]{2,1,0:T(8,128)S(1)}, u32[]{:S(2)}, u32[]{:S(2)}) collective-permute-start(f32[1,40,256]{2,1,0:T(8,128)} %param.14), channel_id=1, source_target_pairs={{0,4},{4,8},{8,12},{12,16},{16,20},{20,24},{24,28},{28,32},{32,36}... | collective-permute-start | bytes 122888 | tf_op jit(solution)/shard_map/ppermute | solution.py:23
  8.5 76.5 %collective-permute-start.2 = (f32[1,40,256]{2,1,0:T(8,128)}, f32[1,40,256]{2,1,0:T(8,128)S(1)}, u32[]{:S(2)}, u32[]{:S(2)}) collective-permute-start(f32[1,40,256]{2,1,0:T(8,128)} %param.14), channel_id=1, source_target_pairs={{4,0},{8,4},{12,8},{16,12},{20,16},{24,20},{28,24},{32,28},{36,32}... | collective-permute-start | bytes 122888 | tf_op jit(solution)/shard_map/ppermute | solution.py:23
  10.5 74.6 %collective-permute-start.3 = (f32[1,40,256]{2,1,0:T(8,128)}, f32[1,40,256]{2,1,0:T(8,128)S(1)}, u32[]{:S(2)}, u32[]{:S(2)}) collective-permute-start(f32[1,40,256]{2,1,0:T(8,128)} %param.14), channel_id=1, source_target_pairs={{8,0},{12,4},{16,8},{20,12},{24,16},{28,20},{32,24},{36,28},{40,32... | collective-permute-start | bytes 122888 | tf_op jit(solution)/shard_map/ppermute | solution.py:23
  91.2 1.0 copy-start.1
  91.2 1.1 copy-start.3
  91.2 1.1 copy-start.10
  91.2 1.3 copy-start
  92.3 0.8 copy-start.9
  92.3 1.2 copy-start.2
  93.5 0.8 copy-start.8
  94.3 12.2 %collective-permute-start.4 = (f32[1,40,256]{2,1,0:T(8,128)S(1)}, f32[1,40,256]{2,1,0:T(8,128)S(1)}, u32[]{:S(2)}, u32[]{:S(2)}) collective-permute-start(f32[1,40,256]{2,1,0:T(8,128)S(1)} %bitcast_add_fusion.7), channel_id=1, source_target_pairs={{0,8},{4,12},{8,16},{12,20},{16,24},{20,28},{24,32},{28,36},{32,40... | collective-permute-start | bytes 122888 | tf_op jit(solution)/shard_map/ppermute | solution.py:23
  95.6 10.9 %collective-permute-start.5 = (f32[1,40,256]{2,1,0:T(8,128)S(1)}, f32[1,40,256]{2,1,0:T(8,128)S(1)}, u32[]{:S(2)}, u32[]{:S(2)}) collective-permute-start(f32[1,40,256]{2,1,0:T(8,128)S(1)} %bitcast_add_fusion.7), channel_id=1, source_target_pairs={{0,4},{4,8},{8,12},{12,16},{16,20},{20,24},{24,28},{28,32},{32,36}... | collective-permute-start | bytes 122888 | tf_op jit(solution)/shard_map/ppermute | solution.py:23
  103.0 5.3 %collective-permute-start.6 = (f32[1,40,256]{2,1,0:T(8,128)S(1)}, f32[1,40,256]{2,1,0:T(8,128)S(1)}, u32[]{:S(2)}, u32[]{:S(2)}) collective-permute-start(f32[1,40,256]{2,1,0:T(8,128)S(1)} %bitcast_add_fusion.7), channel_id=1, source_target_pairs={{4,0},{8,4},{12,8},{16,12},{20,16},{24,20},{28,24},{32,28},{36,32}... | collective-permute-start | bytes 122888 | tf_op jit(solution)/shard_map/ppermute | solution.py:23
  105.0 4.7 %collective-permute-start.7 = (f32[1,40,256]{2,1,0:T(8,128)S(1)}, f32[1,40,256]{2,1,0:T(8,128)S(1)}, u32[]{:S(2)}, u32[]{:S(2)}) collective-permute-start(f32[1,40,256]{2,1,0:T(8,128)S(1)} %bitcast_add_fusion.7), channel_id=1, source_target_pairs={{8,0},{12,4},{16,8},{20,12},{24,16},{28,20},{32,24},{36,28},{40,32... | collective-permute-start | bytes 122888 | tf_op jit(solution)/shard_map/ppermute | solution.py:23
  119.4 65.7 %copy-start.4 = (f32[1,8,40,256]{3,2,1,0:T(8,128)S(1)}, f32[1,8,40,256]{3,2,1,0:T(8,128)}, u32[]{:S(2)}) copy-start(f32[1,8,40,256]{3,2,1,0:T(8,128)} %param.16) | copy-start | bytes 983044
  186.3 12.1 %collective-permute-start.8 = (f32[1,40,256]{2,1,0:T(8,128)S(1)}, f32[1,40,256]{2,1,0:T(8,128)S(1)}, u32[]{:S(2)}, u32[]{:S(2)}) collective-permute-start(f32[1,40,256]{2,1,0:T(8,128)S(1)} %bitcast_add_fusion.5), channel_id=1, source_target_pairs={{0,8},{4,12},{8,16},{12,20},{16,24},{20,28},{24,32},{28,36},{32,40... | collective-permute-start | bytes 122888 | tf_op jit(solution)/shard_map/ppermute | solution.py:23
  189.9 8.5 %collective-permute-start.9 = (f32[1,40,256]{2,1,0:T(8,128)S(1)}, f32[1,40,256]{2,1,0:T(8,128)S(1)}, u32[]{:S(2)}, u32[]{:S(2)}) collective-permute-start(f32[1,40,256]{2,1,0:T(8,128)S(1)} %bitcast_add_fusion.5), channel_id=1, source_target_pairs={{0,4},{4,8},{8,12},{12,16},{16,20},{20,24},{24,28},{28,32},{32,36}... | collective-permute-start | bytes 122888 | tf_op jit(solution)/shard_map/ppermute | solution.py:23
  195.0 5.3 %collective-permute-start.10 = (f32[1,40,256]{2,1,0:T(8,128)S(1)}, f32[1,40,256]{2,1,0:T(8,128)S(1)}, u32[]{:S(2)}, u32[]{:S(2)}) collective-permute-start(f32[1,40,256]{2,1,0:T(8,128)S(1)} %bitcast_add_fusion.5), channel_id=1, source_target_pairs={{4,0},{8,4},{12,8},{16,12},{20,16},{24,20},{28,24},{32,28},{36,32}... | collective-permute-start | bytes 122888 | tf_op jit(solution)/shard_map/ppermute | solution.py:23
  196.9 5.8 %collective-permute-start.11 = (f32[1,40,256]{2,1,0:T(8,128)S(1)}, f32[1,40,256]{2,1,0:T(8,128)S(1)}, u32[]{:S(2)}, u32[]{:S(2)}) collective-permute-start(f32[1,40,256]{2,1,0:T(8,128)S(1)} %bitcast_add_fusion.5), channel_id=1, source_target_pairs={{8,0},{12,4},{16,8},{20,12},{24,16},{28,20},{32,24},{36,28},{40,32... | collective-permute-start | bytes 122888 | tf_op jit(solution)/shard_map/ppermute | solution.py:23
  213.1 68.6 %copy-start.5 = (f32[1,8,40,256]{3,2,1,0:T(8,128)S(1)}, f32[1,8,40,256]{3,2,1,0:T(8,128)}, u32[]{:S(2)}) copy-start(f32[1,8,40,256]{3,2,1,0:T(8,128)} %param.16) | copy-start | bytes 983044
  213.1 68.6 %copy-start.6 = (f32[40,8,256]{2,0,1:T(8,128)S(1)}, f32[40,8,256]{2,0,1:T(8,128)}, u32[]{:S(2)}) copy-start(f32[40,8,256]{2,0,1:T(8,128)} %copy.41) | copy-start | bytes 983044
  284.1 11.3 %collective-permute-start.12 = (f32[1,40,256]{2,1,0:T(8,128)S(1)}, f32[1,40,256]{2,1,0:T(8,128)S(1)}, u32[]{:S(2)}, u32[]{:S(2)}) collective-permute-start(f32[1,40,256]{2,1,0:T(8,128)S(1)} %bitcast_add_fusion.3), channel_id=1, source_target_pairs={{0,8},{4,12},{8,16},{12,20},{16,24},{20,28},{24,32},{28,36},{32,40... | collective-permute-start | bytes 122888 | tf_op jit(solution)/shard_map/ppermute | solution.py:23
  287.1 8.4 %collective-permute-start.13 = (f32[1,40,256]{2,1,0:T(8,128)S(1)}, f32[1,40,256]{2,1,0:T(8,128)S(1)}, u32[]{:S(2)}, u32[]{:S(2)}) collective-permute-start(f32[1,40,256]{2,1,0:T(8,128)S(1)} %bitcast_add_fusion.3), channel_id=1, source_target_pairs={{0,4},{4,8},{8,12},{12,16},{16,20},{20,24},{24,28},{28,32},{32,36}... | collective-permute-start | bytes 122888 | tf_op jit(solution)/shard_map/ppermute | solution.py:23
  292.2 5.3 %collective-permute-start.14 = (f32[1,40,256]{2,1,0:T(8,128)S(1)}, f32[1,40,256]{2,1,0:T(8,128)S(1)}, u32[]{:S(2)}, u32[]{:S(2)}) collective-permute-start(f32[1,40,256]{2,1,0:T(8,128)S(1)} %bitcast_add_fusion.3), channel_id=1, source_target_pairs={{4,0},{8,4},{12,8},{16,12},{20,16},{24,20},{28,24},{32,28},{36,32}... | collective-permute-start | bytes 122888 | tf_op jit(solution)/shard_map/ppermute | solution.py:23
  294.2 5.8 %collective-permute-start.15 = (f32[1,40,256]{2,1,0:T(8,128)S(1)}, f32[1,40,256]{2,1,0:T(8,128)S(1)}, u32[]{:S(2)}, u32[]{:S(2)}) collective-permute-start(f32[1,40,256]{2,1,0:T(8,128)S(1)} %bitcast_add_fusion.3), channel_id=1, source_target_pairs={{8,0},{12,4},{16,8},{20,12},{24,16},{28,20},{32,24},{36,28},{40,32... | collective-permute-start | bytes 122888 | tf_op jit(solution)/shard_map/ppermute | solution.py:23
  306.0 44.7 %copy-start.7 = (f32[1,8,40,256]{3,2,1,0:T(8,128)S(1)}, f32[1,8,40,256]{3,2,1,0:T(8,128)}, u32[]{:S(2)}) copy-start(f32[1,8,40,256]{3,2,1,0:T(8,128)} %get-tuple-element.12) | copy-start | bytes 983044
where the time goes:
time: 354 us; the launch traced here: 351 us
  blocking collectives  215 us (61%)
  starting transfers between devices  46.2 us (13%)
  local copies, waits for them, and re-layouts  38 us (11%)
  between operations  24.9 us (7%)
  other arithmetic  13.9 us (4%)
  waiting for transfers between devices  11.8 us (3%)
    all_gather x8, blocking collectives, all_in_one(): both, at, found = (lax.all_gather(jnp.concatenate(lines), axis), 0, {})  103 us
    psum x4, blocking collectives, over_axes(): return functools.reduce(lax.psum, axes, x)  69.2 us
    ppermute x16, starting transfers between devices, shifted(): lax.ppermute(value, axis, [(source, source + steps) for source in range(f...  46.2 us
    pmax x4, blocking collectives, by_axis(): return functools.reduce(lax.pmax, axes, x)  42.9 us
    gather x4, local copies, waits for them, and re-layouts, lookup(): jnp.take(joined[0], column, axis=1)  26.1 us
    ppermute x16, waiting for transfers between devices, shifted(): lax.ppermute(value, axis, [(source, source + steps) for source in range(f...  11.8 us
  transfers between devices with their start and end apart: 16, of which 6 were waited for; matrix products, arithmetic and copies ran while one was open for 1% of the time, Pallas kernels for 0%

commit v1 on v0

v1 whole, which is shorter than its diff:
```python
import functools

import jax
import jax.numpy as jnp
from jax import lax
from jax.experimental import pallas as pl
from jax.experimental.pallas import tpu as pltpu
from jax.sharding import Mesh
from jax.sharding import PartitionSpec as P

Z, X, Y = 8, 4, 4
BLOCKS = Z * X * 2
NB = 256
T = 40
DEGREE = 8
NPLAT = 128
ITERS = 3
RHO = 0.5
KAPPA = 0.5
TILES = T // 8
PEERS = 15
OFFS = (-2, -1, 1, 2)
AGENTS = ("agents_0", "agents_1", "agents_2")
MESH = pl.DeviceIdType.MESH
F32 = jnp.float32
HALVES = (slice(0, 128), slice(128, 256))


def kernel(
    q_h, inv_h, pre_h, free_h, off_h, lam_h, own_h, slot_h, plat_h,
    plan_o, lam_o,
    q_v, inv_b, pre_b, off_v, lam_v, gap_v, near_v, own_v, slot_v, plat_v,
    col_v, low_v, hot_v, inv_f, pre_f, traj_v, nbr_v, c0_v, c1_v, vec_v, plan_v, att_v, div_v,
    s_buf, a_buf, m_buf, b_buf, e_buf, c_buf, p_src, p1_buf, p2_buf,
    in_sem, out_sem, nbr_ss, nbr_rs, a_ss, a_rs, b_ss, b_rs, c_ss, c_rs, p_ss, p_rs,
):
    z = lax.axis_index("agents_0")
    x = lax.axis_index("agents_1")
    core = lax.axis_index("agents_2")
    y = lax.axis_index("group")
    mine = (z * X + x) * 2 + core
    u = z * 2 + core
    v = x * Y + y

    loads = [
        pltpu.make_async_copy(src, dst, in_sem.at[i])
        for i, (src, dst) in enumerate(
            (
                (free_h, traj_v.at[0]),
                (plat_h, plat_v),
                (own_h, own_v),
                (slot_h, slot_v),
                (off_h, off_v),
                (lam_h, lam_v),
                (pre_h, pre_b),
                (q_h, q_v),
                (inv_h, inv_b),
            )
        )
    ]
    for load in loads:
        load.start()

    def at_block(b):
        return {"agents_0": b // (2 * X), "agents_1": (b // 2) % X, "agents_2": b % 2}

    def at_u(w):
        return {"agents_0": w // 2, "agents_2": w % 2}

    def at_v(w):
        return {"agents_1": w // Y, "group": w % Y}

    near_ids = [at_block(lax.rem(mine - d + BLOCKS, BLOCKS)) for d in OFFS]
    u_ids = [at_u(lax.rem(u + d, 16)) for d in range(1, 16)]
    v_ids = [at_v(lax.rem(v + d, 16)) for d in range(1, 16)]

    barrier = pltpu.get_barrier_semaphore()
    for ids in near_ids + u_ids + v_ids:
        pl.semaphore_signal(barrier, inc=1, device_id=ids, device_id_type=MESH)

    def remote(src, dst, ss, rs, ids):
        return pltpu.make_async_remote_copy(
            src_ref=src, dst_ref=dst, send_sem=ss, recv_sem=rs, device_id=ids, device_id_type=MESH
        )

    def whole_wait(ref, sem):
        pltpu.make_async_copy(ref, ref, sem).wait()

    def nbr_send(i):
        for j, ids in enumerate(near_ids):
            remote(traj_v.at[i], nbr_v.at[i, j], nbr_ss.at[i, j], nbr_rs.at[i, j], ids).start()

    def platoon_tiles(i):
        field = traj_v[i]
        hi = field.astype(jnp.bfloat16)
        rest = field - hi.astype(F32)
        mid = rest.astype(jnp.bfloat16)
        low = (rest - mid.astype(F32)).astype(jnp.bfloat16)
        total = jnp.zeros((T, NPLAT), F32)
        for part in (low, mid, hi):
            total += lax.dot_general(
                part, hot_v[...], (((1,), (1,)), ((), ())), preferred_element_type=F32
            )
        for g in range(TILES):
            s_buf[i, g] = total[8 * g : 8 * g + 8]

    def owner_of(tiles):
        return jnp.logical_and(core == 1, z < tiles)

    def sum_send(i, tiles):
        for g in range(tiles):
            owner = 2 * g + 1

            @pl.when(u != owner)
            def _():
                slot = lax.rem(u - owner + 16, 16) - 1
                remote(
                    s_buf.at[i, g], a_buf.at[i, slot], a_ss.at[i, g], a_rs.at[i],
                    {"agents_0": g, "agents_2": 1},
                ).start()

    def sum_mid(i, tiles):
        @pl.when(owner_of(tiles))
        def _():
            whole_wait(a_buf.at[i], a_rs.at[i])
            m_buf[i] = s_buf[i, z] + jnp.sum(a_buf[i], axis=0)
            for d in range(PEERS):
                remote(m_buf.at[i], b_buf.at[i, d], b_ss.at[i], b_rs.at[i], v_ids[d]).start()

    def sum_end(i, tiles):
        @pl.when(owner_of(tiles))
        def _():
            whole_wait(b_buf.at[i], b_rs.at[i])
            total = m_buf[i] + jnp.sum(b_buf[i], axis=0)
            e_buf[i] = total
            c_buf[i, z] = total
            for d in range(PEERS):
                remote(e_buf.at[i], c_buf.at[i, z], c_ss.at[i], c_rs.at[i, z], u_ids[d]).start()

        for g in range(tiles):

            @pl.when(u != 2 * g + 1)
            def _():
                whole_wait(c_buf.at[i, g], c_rs.at[i, g])

    def sum_drain(i, tiles):
        for g in range(tiles):

            @pl.when(u != 2 * g + 1)
            def _():
                whole_wait(s_buf.at[i, g], a_ss.at[i, g])

        @pl.when(owner_of(tiles))
        def _():
            whole_wait(b_buf.at[i], b_ss.at[i])
            whole_wait(a_buf.at[i], c_ss.at[i])

    def peak_first(i, peak):
        p_src[i, 0] = peak
        for d in range(PEERS):
            remote(p_src.at[i, 0], p1_buf.at[i, d], p_ss.at[i, 0], p_rs.at[i, 0], u_ids[d]).start()

    def peak_second(i):
        whole_wait(p1_buf.at[i], p_rs.at[i, 0])
        p_src[i, 1] = jnp.maximum(p_src[i, 0], jnp.max(p1_buf[i], axis=0))
        for d in range(PEERS):
            remote(p_src.at[i, 1], p2_buf.at[i, d], p_ss.at[i, 1], p_rs.at[i, 1], v_ids[d]).start()

    def peak_end(i):
        whole_wait(p2_buf.at[i], p_rs.at[i, 1])
        peak = jnp.maximum(p_src[i, 1], jnp.max(p2_buf[i], axis=0))
        return 1.0 / (1.0 + jnp.max(peak, axis=1, keepdims=True))

    def peak_drain(i):
        whole_wait(p1_buf.at[i], p_ss.at[i, 0])
        whole_wait(p2_buf.at[i], p_ss.at[i, 1])

    def row(ref, k, half):
        return jnp.concatenate([ref[k, :, half]] * TILES, axis=0)

    def pick(src, block, col, low, other):
        first = jnp.take_along_axis(src[0], low, axis=1, mode="promise_in_bounds")
        second = jnp.take_along_axis(src[1], low, axis=1, mode="promise_in_bounds")
        return jnp.where(col == 2 * block, first, jnp.where(col == 2 * block + 1, second, other))

    def look(ref, block, fresh):
        src = [ref[:, half] for half in HALVES]

        def body(k, carry):
            for half in HALVES:
                other = 0.0 if fresh else near_v[k, :, half]
                near_v[k, :, half] = pick(src, block, row(col_v, k, half), row(low_v, k, half), other)
            return carry

        lax.fori_loop(0, DEGREE, body, 0)

    def gather_all(i, s_prev):
        look(traj_v.at[i], 2, True)
        for j, block in ((1, 1), (2, 3), (0, 0)):
            whole_wait(nbr_v.at[i, j], nbr_rs.at[i, j])
            look(nbr_v.at[i, j], block, False)
        whole_wait(nbr_v.at[i, 3], nbr_rs.at[i, 3])
        src = [nbr_v[i, 3, :, half] for half in HALVES]
        top = jnp.zeros((T, 128), F32)
        zero = jnp.zeros((T, 128), F32)
        for half in HALVES:
            here = traj_v[i, :, half]

            def body(k, carry):
                c0, c1, top = carry
                col = row(col_v, k, half)
                near = pick(src, 4, col, row(low_v, k, half), near_v[k, :, half])
                off = off_v[k, :, half]
                lam = lam_v[k, :, half]
                if i > 1:
                    lam = lam + s_prev * gap_v[k, :, half]
                    lam_v[k, :, half] = lam
                live = col >= 0
                c0 = c0 + jnp.where(live, lam - RHO * (near + off), 0.0)
                if i > 0:
                    gap = jnp.where(live, here - near - off, 0.0)
                    gap_v[k, :, half] = gap
                    c1 = c1 + gap
                    top = jnp.maximum(top, jnp.abs(gap))
                return c0, c1, top

            c0, c1, top = lax.fori_loop(0, DEGREE, body, (zero, zero, top))
            c0_v[:, half] = c0
            c1_v[:, half] = c1
        return jnp.max(top, axis=0, keepdims=True)

    def contract(mat, vec):
        def body(g, acc):
            at = pl.multiple_of(g * 8, 8)
            part = vec[pl.ds(at, 8), :]
            for r in range(8):
                acc = acc + mat[at + r] * part[r : r + 1]
            return acc

        return lax.fori_loop(0, TILES, body, jnp.zeros((T, NB), F32))

    def predict(i):
        plan = plan_v[...]

        def body(g, carry):
            at = pl.multiple_of(g * 8, 8)
            rows = [jnp.sum(pre_f[at + r] * plan, axis=0, keepdims=True) for r in range(8)]
            traj_v[i, pl.ds(at, 8), :] = jnp.concatenate(rows, axis=0) + traj_v[0, pl.ds(at, 8), :]
            return carry

        lax.fori_loop(0, TILES, body, 0)

    def attract(i):
        for half in HALVES:
            index = jnp.broadcast_to(plat_v[:, half], (T, 128))
            means = c_buf[i, 0:TILES].reshape(T, NPLAT) / div_v[...]
            att_v[:, half] = jnp.take_along_axis(means, index, axis=1, mode="promise_in_bounds")

    loads[0].wait()
    pl.semaphore_wait(barrier, len(near_ids) + 2 * PEERS)
    nbr_send(0)
    loads[1].wait()
    match = lax.broadcasted_iota(jnp.int32, (NPLAT, NB), 0) == plat_v[...]
    hot_v[...] = match.astype(F32).astype(jnp.bfloat16)
    ones = jnp.ones((8, NB), jnp.bfloat16)
    s_buf[0, TILES] = lax.dot_general(
        ones, hot_v[...], (((1,), (1,)), ((), ())), preferred_element_type=F32
    )
    platoon_tiles(0)
    sum_send(0, TILES + 1)
    loads[2].wait()
    loads[3].wait()
    slot = slot_v[...]
    low = slot & 127
    col = jnp.where(slot >= 0, (own_v[...] - mine + 2) * 2 + (slot >> 7), -1)
    for k in range(DEGREE):
        low_v[k] = jnp.broadcast_to(low[k : k + 1], (8, NB))
        col_v[k] = jnp.broadcast_to(col[k : k + 1], (8, NB))
    loads[4].wait()
    loads[5].wait()
    gather_all(0, None)
    sum_mid(0, TILES + 1)
    for load in loads[6:]:
        load.wait()

    def widen(t, carry):
        inv_f[t] = inv_b[t].astype(F32)
        pre_f[t] = pre_b[t].astype(F32)
        return carry

    lax.fori_loop(0, T, widen, 0)
    sum_end(0, TILES + 1)
    div_v[...] = jnp.broadcast_to(jnp.maximum(c_buf[0, TILES, 0:1], 1.0), (T, NPLAT))
    attract(0)

    s = None
    for step in range(ITERS):
        i = step + 1
        more = i < ITERS
        coupling = c0_v[...] - KAPPA * att_v[...]
        if step > 0:
            coupling = coupling + s * c1_v[...]
        vec_v[...] = coupling
        vec_v[...] = q_v[...] + contract(pre_f, vec_v)
        plan_v[...] = -contract(inv_f, vec_v)
        predict(i)
        nbr_send(i)
        if more:
            platoon_tiles(i)
            sum_send(i, TILES)
        else:
            pltpu.make_async_copy(plan_v, plan_o, out_sem.at[DEGREE]).start()
        peak = gather_all(i, s)
        peak_first(step, peak)
        if more:
            sum_mid(i, TILES)
        peak_second(step)
        if more:
            sum_end(i, TILES)
            attract(i)
        s = peak_end(step)

    for k in range(DEGREE):
        lam_v[k] = lam_v[k] + s * gap_v[k]
        pltpu.make_async_copy(lam_v.at[k], lam_o.at[k], out_sem.at[k]).start()
    for i in range(ITERS + 1):
        for j in range(len(OFFS)):
            whole_wait(traj_v.at[i], nbr_ss.at[i, j])
    for i in range(ITERS):
        sum_drain(i, TILES + 1 if i == 0 else TILES)
        peak_drain(i)
    for k in range(DEGREE):
        pltpu.make_async_copy(lam_v.at[k], lam_o.at[k], out_sem.at[k]).wait()
    pltpu.make_async_copy(plan_v, plan_o, out_sem.at[DEGREE]).wait()


def local(q_lin, inverse, predict, free_traj, offsets, multipliers, nbr_owner, nbr_slot, platoon):
    vm = pltpu.VMEM
    i32, bf16 = jnp.int32, jnp.bfloat16
    dma = pltpu.SemaphoreType.DMA
    field = (T, NB)
    slots = (DEGREE, T, NB)
    mats = (T, T, NB)
    plan, lam = pl.pallas_call(
        kernel,
        out_shape=(jax.ShapeDtypeStruct(field, F32), jax.ShapeDtypeStruct(slots, F32)),
        in_specs=[pl.BlockSpec(memory_space=pl.ANY)] * 9,
        out_specs=(pl.BlockSpec(memory_space=pl.ANY), pl.BlockSpec(memory_space=pl.ANY)),
        scratch_shapes=[
            vm(field, F32), vm(mats, bf16), vm(mats, bf16), vm(slots, F32), vm(slots, F32),
            vm(slots, F32), vm(slots, F32), vm((DEGREE, NB), i32), vm((DEGREE, NB), i32), vm((1, NB), i32),
            vm((DEGREE, 8, NB), i32), vm((DEGREE, 8, NB), i32), vm((NPLAT, NB), bf16), vm(mats, F32), vm(mats, F32),
            vm((ITERS + 1, T, NB), F32), vm((ITERS + 1, 4, T, NB), F32),
            vm(field, F32), vm(field, F32), vm(field, F32), vm(field, F32), vm(field, F32), vm((T, NPLAT), F32),
            vm((ITERS, TILES + 1, 8, 128), F32), vm((ITERS, PEERS, 8, 128), F32), vm((ITERS, 8, 128), F32),
            vm((ITERS, PEERS, 8, 128), F32), vm((ITERS, 8, 128), F32), vm((ITERS, TILES + 1, 8, 128), F32),
            vm((ITERS, 2, 1, 128), F32), vm((ITERS, PEERS, 1, 128), F32), vm((ITERS, PEERS, 1, 128), F32),
            dma((9,)), dma((DEGREE + 1,)), dma((ITERS + 1, 4)), dma((ITERS + 1, 4)),
            dma((ITERS, TILES + 1)), dma((ITERS,)), dma((ITERS,)), dma((ITERS,)), dma((ITERS,)),
            dma((ITERS, TILES + 1)), dma((ITERS, 2)), dma((ITERS, 2)),
        ],
        compiler_params=pltpu.CompilerParams(collective_id=0, has_side_effects=True),
        name="consensus",
    )(
        q_lin[0], inverse[0], predict[0], free_traj[0], offsets[0], multipliers[0],
        nbr_owner[0], nbr_slot[0], platoon,
    )
    return plan[None], lam[None]


def solution(mesh):
    finer = Mesh(
        mesh.devices.reshape(Z, X, 2, mesh.shape["group"]),
        ("agents_0", "agents_1", "agents_2", "group"),
    )
    placed = (
        P("group", None, AGENTS),
        P("group", None, None, AGENTS),
        P("group", None, None, AGENTS),
        P("group", None, AGENTS),
        P("group", None, None, AGENTS),
        P("group", None, None, AGENTS),
        P("group", None, AGENTS),
        P("group", None, AGENTS),
        P("group", AGENTS),
    )
    return jax.shard_map(
        local,
        mesh=finer,
        in_specs=placed,
        out_specs=(P("group", None, AGENTS), P("group", None, None, AGENTS)),
        check_vma=False,
    )
```

time: 354 us -> 80.2 us (0.23)
  blocking collectives: 215 us -> 0 us
  Pallas kernels: 0 us -> 76.3 us
  starting transfers between devices: 46.2 us -> 0 us
  local copies, waits for them, and re-layouts: 38 us -> 3.12 us
  between operations: 24.9 us -> 0.64 us
  other arithmetic: 13.9 us -> 0 us
  waiting for transfers between devices: 11.8 us -> 0 us
    all_gather x8 -> x0, blocking collectives: 103 us -> none  [all_in_one(): both, at, found = (lax.all_gather(jnp.concatenate(lines), axis), 0, {})]
    pallas_call x0 -> x1, Pallas kernels: none -> 76.3 us  [local(): pl.pallas_call(kernel, out_shape=(jax.ShapeDtypeStruct(field, F32), jax.S...]
    psum x4 -> x0, blocking collectives: 69.2 us -> none  [over_axes(): return functools.reduce(lax.psum, axes, x)]
    ppermute x16 -> x0, starting transfers between devices: 46.2 us -> none  [shifted(): lax.ppermute(value, axis, [(source, source + steps) for source in range(f...]
    pmax x4 -> x0, blocking collectives: 42.9 us -> none  [by_axis(): return functools.reduce(lax.pmax, axes, x)]
    gather x4 -> x0, local copies, waits for them, and re-layouts: 26.1 us -> none  [lookup(): jnp.take(joined[0], column, axis=1)]
    ppermute x16 -> x0, waiting for transfers between devices: 11.8 us -> none  [shifted(): lax.ppermute(value, axis, [(source, source + steps) for source in range(f...]
    slice x16 -> x0, local copies, waits for them, and re-layouts: 4.81 us -> none  [the longest x8 4.79 us: joined_all(): x = combine(x, jax.tree.map(lambda part: part[k], pieces))]
  transfers between devices with their start and end apart: 16 -> 0, of which waited for: 6 -> 0; matrix products, arithmetic and copies ran while one was open for 1% -> 0% of each run, Pallas kernels for 0% -> 0%
where the time goes in v1:
time: 80.2 us; the launch traced here: 80 us
  Pallas kernels  76.3 us (95%)
  local copies, waits for them, and re-layouts  3.12 us (4%)
    pallas_call x1, Pallas kernels, local(): pl.pallas_call(kernel, out_shape=(jax.ShapeDtypeStruct(field, F32), jax.S...  76.3 us
    unnamed x2, local copies, waits for them, and re-layouts  3.12 us

profile of v1, /device:TPU:1, one launch (start us, length us, event | category | flops | bytes accessed | tf_op | source)
XLA Modules:
  0.0 80.0 jit_solution(5965808539223618354)
XLA Ops:
  0.6 76.3 %consensus.1 = (f32[40,256]{1,0:T(8,128)}, f32[8,40,256]{2,1,0:T(8,128)}) custom-call(f32[40,256]{1,0:T(8,128)} %bitcast.16, bf16[40,40,256]{2,1,0:T(8,128)(2,1)} %bitcast.10, bf16[40,40,256]{2,1,0:T(8,128)(2,1)} %bitcast.11, f32[40,256]{1,0:T(8,128)} %bitcast.17, f32[8,40,256]{2,1,0:T(8,128)} %bitcast.13, f32[8,40,256]{2,1,0:T(8,128)} %bitcast.14, ...), custom_call_target="tpu_custom_call" | custom-call | tf_op jit(solution)/shard_map/consensus/pallas_call | solution.py:344
  76.9 1.4 %copy.13 = f32[1,40,256]{2,1,0:T(8,128)} copy(f32[1,40,256]{2,1,0:T(8,128)} %bitcast.15) | data formatting | bytes 81920
  78.3 1.7 %copy.14 = f32[1,8,40,256]{3,2,1,0:T(8,128)} copy(f32[1,8,40,256]{3,2,1,0:T(8,128)} %bitcast.12) | data formatting | bytes 655360
